TPU v7x, 32 devices: a whole 2x2x4 slice. The times are simulated.
32 devices in a mesh: grp: 2 (over core), dev: 16 (over z, y, x).
Axes of the slice: x: 2, y: 2, z: 4, core: 2. Of those that a mesh axis runs over, the one named last changes fastest.
Arguments:
- tokens: bfloat16 [2048, 2048], P('dev', 'grp'), may hold values from -6 to 6
- gate_up: bfloat16 [2048, 2, 16, 7168], P('dev', None, None, 'grp'), may hold values from -0.125 to 0.125
- down: bfloat16 [16, 7168, 2048], P('dev', 'grp'), may hold values from -0.046875 to 0.046875
- expert_ids: int32 [2048, 2], P('dev'), may hold values from 0 to 7, all different within a row; in each aligned block of 128 rows (0 to 127, 128 to 255, ...) at most 40 rows name the same one
- gate_num: int32 [2048, 2], P('dev'), may hold values from 1 to 15
Outputs:
- moe_out: bfloat16 [2048, 2048], P('dev', 'grp')
Inputs may be any that keep to these rules, and one draw needn't show every extreme that they name: `expert_ids`: each row names 2 different experts. In each aligned block of 128 rows no expert is named by more than 40 rows, a bound that some block reaches.
All inputs are finite; a program needn't handle non-finite values.
Results may differ from a plain program's by a relative error of at most 0.0083.
Values may be sent and summed in bfloat16 or wider, within the bound.
A program may use at most 192 MiB of HBM per device.

v0:
```python
import jax
import jax.numpy as jnp
from jax import lax
from jax.sharding import PartitionSpec as P

EXPERTS = 8
TOP = 2
CAP = 40


def local(tokens, gate_up, down, expert_ids, gate_num):
    shards = lax.axis_size("dev")
    column_count = shards // EXPERTS
    tok_rows = tokens.shape[0]
    half_width = tokens.shape[1]
    hidden_width = gate_up.shape[3]
    flat_ids = expert_ids.reshape(-1)
    onehot = (flat_ids[:, None] == jnp.arange(EXPERTS, dtype=jnp.int32)[None, :]).astype(jnp.int32)
    earlier = jnp.cumsum(onehot, axis=0) - onehot
    slot_index = jnp.sum(earlier * onehot, axis=1)
    positions = (flat_ids * CAP + slot_index).reshape(tok_rows, TOP)
    numerators = gate_num.astype(jnp.float32)
    shares = numerators / jnp.sum(numerators, axis=1, keepdims=True)
    places = jnp.arange(EXPERTS * CAP, dtype=jnp.int32)
    matches = places[:, None, None] == positions[None, :, :]
    select = jnp.any(matches, axis=2).astype(jnp.bfloat16)
    combine = jnp.sum(jnp.where(matches, shares[None, :, :], 0.0), axis=2)

    def make_project(row_block):

        def project(received_block):
            block_cols = received_block.shape[3]
            activity = jnp.dot(
                row_block,
                received_block.reshape(received_block.shape[0], 2 * block_cols),
                preferred_element_type=jnp.float32,
            )
            return (jax.nn.silu(activity[:, :block_cols]) * activity[:, block_cols:]).astype(
                jnp.bfloat16
            )

        return project

    outgoing = jnp.dot(select, tokens, preferred_element_type=jnp.float32).astype(jnp.bfloat16)
    feature_count = outgoing.shape[1]
    copies = jnp.broadcast_to(
        outgoing.reshape(EXPERTS, 1, CAP, feature_count),
        (EXPERTS, column_count, CAP, feature_count),
    )
    received = lax.all_to_all(
        copies.reshape(shards, CAP, feature_count), "dev", split_axis=0, concat_axis=0, tiled=True
    )
    arrived = lax.all_gather(received, "grp", axis=2, tiled=True)
    feature_total = arrived.shape[2]
    expert_rows = arrived.reshape(shards * CAP, feature_total)
    project = make_project(expert_rows)
    columns_in = lax.all_to_all(gate_up, "dev", split_axis=2, concat_axis=0, tiled=True)
    hidden = project(columns_in)
    partial_value = jnp.dot(
        hidden, down.reshape(hidden_width, feature_total), preferred_element_type=jnp.float32
    )
    summed = lax.psum_scatter(partial_value, "grp", scatter_dimension=1, tiled=True)
    returned = lax.all_to_all(
        summed.reshape(shards, CAP, half_width), "dev", split_axis=0, concat_axis=0, tiled=True
    )
    expert_out = jnp.sum(returned.reshape(EXPERTS, column_count, CAP, half_width), axis=1).reshape(
        EXPERTS * CAP, half_width
    )
    combined = jnp.dot(
        combine.T, expert_out, preferred_element_type=jnp.float32, precision=lax.Precision.HIGHEST
    )
    return combined.astype(jnp.bfloat16)


def solution(mesh):
    in_specs = (
        P("dev", "grp"),
        P("dev", None, None, "grp"),
        P("dev", "grp", None),
        P("dev", None),
        P("dev", None),
    )
    out_specs = P("dev", "grp")
    return jax.shard_map(local, mesh=mesh, in_specs=in_specs, out_specs=out_specs, check_vma=False)
```

profile of v0, /device:TPU:8, one launch (start us, length us, event | category | flops | bytes accessed | tf_op | source)
XLA Modules:
  0.0 898.1 jit_solution(15576072720367284192)
XLA Ops:
  6.5 0.0 copy-start
  6.5 0.8 copy.35
  7.4 0.1 eq.43
  7.5 0.1 eq.39
  7.7 0.6 reduce-window.6
  8.2 0.2 slice_reduce_fusion
  8.5 0.1 fusion.10
  8.6 0.1 reduce_sum.39
  8.7 0.1 copy.37
  8.8 0.7 multiply_add_fusion
  9.6 0.0 copy-done
  9.6 0.3 convolution_convert_fusion
  9.9 1.3 broadcast_in_dim.26
  11.2 7.2 all-to-all-start
  18.4 27.6 %copy.38 = bf16[128,2,16,3584]{3,0,1,2:T(8,128)(2,1)} copy(bf16[128,2,16,3584]{3,2,1,0:T(8,128)(2,1)} %param.6) | data formatting | bytes 58720256 | tf_op args[1]
  46.0 3.9 all-to-all-done
  49.9 1.1 copy-done.2
  50.9 5.7 all-to-all-start.1
  56.6 0.0 all-gather.2.cloned.1.call-start
  56.6 0.7 all-gather.2.cloned.1.call-update
  57.3 0.2 reduce-scatter.2.cloned.1.call-start
  57.6 627.4 %all-to-all-done.1 = bf16[128,2,16,3584]{3,0,1,2:T(8,128)(2,1)} async-done(((bf16[128,2,16,3584]{3,0,1,2:T(8,128)(2,1)}), bf16[128,2,16,3584]{3,0,1,2:T(8,128)(2,1)}, u32[]{:S(2)}, u32[]{:S(2)}) %all-to-all-start.1) | async-done | bytes 29360160 | tf_op jit(solution)/shard_map/all_to_all | solution.py:57
  684.9 39.3 %copy.39 = bf16[16,128,2,1,3584]{1,0,4,2,3:T(8,128)(2,1)} copy(bf16[16,128,2,1,3584]{4,1,2,0,3:T(8,128)(2,1)} %bitcast.6) | data formatting | bytes 58720256 | tf_op jit(solution)/shard_map/all_to_all | solution.py:57
  724.2 26.1 %fusion = f32[640,7168]{1,0:T(8,128)} fusion(bf16[640,2048]{1,0:T(8,128)(2,1)} %bitcast.37, bf16[896,8,16,128]{3,2,1,0:T(8,128)(2,1)} %bitcast.33), kind=kOutput, calls=%fused_computation | convolution fusion | flops 18790481920 | bytes 50331648 | tf_op jit(solution)/shard_map/dot_general | solution.py:33
  750.3 19.5 %fusion.3 = f32[640,2048]{1,0:T(8,128)} fusion(bf16[1,3584,2048]{2,1,0:T(8,128)(2,1)} %param.7, f32[640,7168]{1,0:T(8,128)} %fusion), kind=kOutput, calls=%fused_computation.3 | convolution fusion | flops 9409003520 | bytes 38273024 | tf_op jit(solution)/shard_map/dot_general | solution.py:59
  769.8 0.0 reduce-scatter.2.cloned.1.call-update
  769.9 54.7 %reduce-scatter.2.cloned.1.call-done = f32[640,1024]{1,0:T(8,128)} async-done(((f32[640,2048]{1,0:T(8,128)}), f32[640,1024]{1,0:T(8,128)}) %reduce-scatter.2.cloned.1.call-update) | async-done | bytes 2621456 | tf_op jit(solution)/shard_map/reduce_scatter | solution.py:62
  824.6 7.0 all-to-all-start.2
  831.6 57.6 %all-to-all-done.2 = f32[16,40,1024]{2,1,0:T(8,128)S(1)} async-done(((f32[16,40,1024]{2,1,0:T(8,128)}), f32[16,40,1024]{2,1,0:T(8,128)S(1)}, u32[]{:S(2)}, u32[]{:S(2)}) %all-to-all-start.2) | async-done | bytes 2621472 | tf_op jit(solution)/shard_map/all_to_all | solution.py:63
  889.3 0.2 bitcast_reduce_fusion
  889.5 1.8 convolution_convert_fusion.1
  891.3 0.0 copy-done.1
  (12 shorter events, 0.2 us)
Async XLA Ops:
  6.5 3.0 copy-start
  11.2 38.6 %all-to-all-start = ((bf16[16,40,1024]{2,1,0:T(8,128)(2,1)}), bf16[16,40,1024]{2,1,0:T(8,128)(2,1)S(1)}, u32[]{:S(2)}, u32[]{:S(2)}) async-start(bf16[16,40,1024]{2,1,0:T(8,128)(2,1)} %bitcast.3), calls=%async_computation | async-start | bytes 2621440 | tf_op jit(solution)/shard_map/all_to_all | solution.py:50
  49.9 1.1 copy-start.2
  50.9 634.0 %all-to-all-start.1 = ((bf16[128,2,16,3584]{3,0,1,2:T(8,128)(2,1)}), bf16[128,2,16,3584]{3,0,1,2:T(8,128)(2,1)}, u32[]{:S(2)}, u32[]{:S(2)}) async-start(bf16[128,2,16,3584]{3,0,1,2:T(8,128)(2,1)} %copy.38), calls=%async_computation.1 | async-start | bytes 58720256 | tf_op jit(solution)/shard_map/all_to_all | solution.py:57
  56.6 667.7 %all-gather.2.cloned.1.call-start = ((), (), s32[]{:S(2)}) async-start(), calls=%async_computation.4 | async-start | bytes 3932160 | tf_op jit(solution)/shard_map/all_gather | solution.py:53
  57.3 767.3 %reduce-scatter.2.cloned.1.call-start = ((), (), s32[]{:S(2)}) async-start(), calls=%async_computation.5 | async-start | bytes 7864320 | tf_op jit(solution)/shard_map/reduce_scatter | solution.py:62
  750.3 141.0 %copy-start.1 = (bf16[128,1024]{1,0:T(8,128)(2,1)S(1)}, bf16[128,1024]{1,0:T(8,128)(2,1)}, u32[]{:S(2)}) copy-start(bf16[128,1024]{1,0:T(8,128)(2,1)} %param.5) | copy-start | bytes 786436
  769.8 61.7 %copy-start.3 = (s32[128,2]{0,1:T(2,128)S(1)}, s32[128,2]{0,1:T(2,128)}, u32[]{:S(2)}) copy-start(s32[128,2]{0,1:T(2,128)} %param.9) | copy-start | bytes 3076
  824.6 64.7 %all-to-all-start.2 = ((f32[16,40,1024]{2,1,0:T(8,128)}), f32[16,40,1024]{2,1,0:T(8,128)S(1)}, u32[]{:S(2)}, u32[]{:S(2)}) async-start(f32[16,40,1024]{2,1,0:T(8,128)} %bitcast.35), calls=%async_computation.3 | async-start | bytes 5242880 | tf_op jit(solution)/shard_map/all_to_all | solution.py:63
Sparse Core Ops, SparseCore 0:
  58.9 11.5 all-gather.1
  770.0 54.5 reduce-scatter.1
where the time goes:
time: 902 us; the launch traced here: 898 us
  waiting for transfers between devices  744 us (82%)
  local copies, waits for them, and re-layouts  70.8 us (8%)
  matrix products  47.7 us (5%)
  starting transfers between devices  20.1 us (2%)
  between operations  13.5 us (1%)
    all_to_all x1, waiting for transfers between devices, local(): lax.all_to_all(gate_up, 'dev', split_axis=2, concat_axis=0, tiled=True)  627 us
    all_to_all x1, waiting for transfers between devices, local(): lax.all_to_all(summed.reshape(shards, CAP, half_width), 'dev', split_axis...  57.6 us
    reduce_scatter x1, waiting for transfers between devices, local(): lax.psum_scatter(partial_value, 'grp', scatter_dimension=1, tiled=True)  54.7 us
    all_to_all x1, local copies, waits for them, and re-layouts, local(): lax.all_to_all(gate_up, 'dev', split_axis=2, concat_axis=0, tiled=True)  39.3 us
    unnamed x10, local copies, waits for them, and re-layouts  29.5 us
    dot_general x1, matrix products, project(): jnp.dot(row_block, received_block.reshape(received_block.shape[0], 2 * bl...  26.1 us
    dot_general x1, matrix products, local(): jnp.dot(hidden, down.reshape(hidden_width, feature_total), preferred_elem...  19.5 us
  transfers between devices with their start and end apart: 5, of which 4 were waited for; matrix products, arithmetic and copies ran while one was open for 7% of the time, Pallas kernels for 0%

commit v1 on v0

v1 whole, which is shorter than its diff:
```python
import functools

import jax
import jax.numpy as jnp
from jax import lax
from jax.experimental import pallas as pl
from jax.experimental.pallas import tpu as pltpu
from jax.sharding import PartitionSpec as P

EXPERTS = 8
TOP = 2
CAP = 40
MESH = pl.DeviceIdType.MESH


def expert_kernel(
    n,
    chunks,
    tile,
    routed_ref,
    weights_ref,
    down_ref,
    keep_ref,
    give_ref,
    rows,
    landed,
    down_rows,
    send_sem,
    recv_sem,
    own_sem,
    row_sem,
    row_send_sem,
    row_recv_sem,
    down_sem,
):
    core = lax.axis_index("grp")
    me = lax.axis_index("dev")
    depth = weights_ref.shape[2]
    width = weights_ref.shape[3] // chunks
    half = rows.shape[2]
    total = rows.shape[1]

    barrier = pltpu.get_barrier_semaphore()

    def greet(step, carry):
        pl.semaphore_signal(
            barrier, inc=1, device_id=(core, lax.rem(me + step, n)), device_id_type=MESH
        )
        return carry

    lax.fori_loop(1, n, greet, 0)
    pl.semaphore_signal(barrier, inc=1, device_id=(1 - core, me), device_id_type=MESH)
    pl.semaphore_wait(barrier, n)

    across = pltpu.make_async_remote_copy(
        src_ref=routed_ref,
        dst_ref=rows.at[core],
        send_sem=row_send_sem,
        recv_sem=row_recv_sem,
        device_id=(1 - core, me),
        device_id_type=MESH,
    )
    across.start()
    here = pltpu.make_async_copy(routed_ref, rows.at[core], row_sem)
    here.start()

    def columns(chunk):
        return pl.ds(pl.multiple_of(chunk * width, width), width)

    def place(owner):
        return pl.ds(pl.multiple_of(owner * depth, depth), depth)

    def send_chunk(chunk, carry):
        def send(step, inner):
            target = lax.rem(me + step, n)
            pltpu.make_async_remote_copy(
                src_ref=weights_ref.at[target, :, :, columns(chunk)],
                dst_ref=landed.at[chunk, :, place(me), :],
                send_sem=send_sem.at[chunk],
                recv_sem=recv_sem.at[chunk],
                device_id=(core, target),
                device_id_type=MESH,
            ).start()
            return inner

        lax.fori_loop(1, n, send, 0)
        pltpu.make_async_copy(
            weights_ref.at[me, :, :, columns(chunk)],
            landed.at[chunk, :, place(me), :],
            own_sem.at[chunk],
        ).start()
        return carry

    lax.fori_loop(0, chunks, send_chunk, 0)

    down_copies = []
    for part in range(2):
        side = core if part == 0 else 1 - core
        copy = pltpu.make_async_copy(
            down_ref.at[0, :, pl.ds(pl.multiple_of(side * half, half), half)],
            down_rows.at[part],
            down_sem.at[part],
        )
        copy.start()
        down_copies.append(copy)
    keep_ref[...] = jnp.zeros_like(keep_ref)
    give_ref[...] = jnp.zeros_like(give_ref)
    here.wait()
    across.wait()
    for copy in down_copies:
        copy.wait()

    def others(chunk):
        return landed.at[chunk, :, pl.ds(0, (n - 1) * depth), :]

    def compute(chunk, carry):
        pltpu.make_async_copy(
            landed.at[chunk, :, place(me), :], landed.at[chunk, :, place(me), :], own_sem.at[chunk]
        ).wait()
        pltpu.make_async_copy(others(chunk), others(chunk), recv_sem.at[chunk]).wait()

        def block(index, inner):
            at = pl.ds(pl.multiple_of(index * tile, tile), tile)

            def project(which):
                low = jnp.dot(
                    rows[0, at, :], landed[chunk, which, :half, :], preferred_element_type=jnp.float32
                )
                return low + jnp.dot(
                    rows[1, at, :], landed[chunk, which, half:, :], preferred_element_type=jnp.float32
                )

            gate = project(0)
            up = project(1)
            hidden = (gate / (1.0 + jnp.exp(-gate)) * up).astype(jnp.bfloat16)
            below = pl.ds(pl.multiple_of(chunk * width, width), width)
            keep_ref[at, :] += jnp.dot(
                hidden, down_rows[0, below, :], preferred_element_type=jnp.float32
            )
            give_ref[at, :] += jnp.dot(
                hidden, down_rows[1, below, :], preferred_element_type=jnp.float32
            )
            return inner

        return lax.fori_loop(0, total // tile, block, carry)

    lax.fori_loop(0, chunks, compute, 0)

    def finish(chunk, carry):
        pltpu.make_async_copy(others(chunk), others(chunk), send_sem.at[chunk]).wait()
        return carry

    lax.fori_loop(0, chunks, finish, 0)


def chunk_count(width):
    for count in (7, 4, 2):
        if width % (count * 128) == 0:
            return count
    return 1


def local(tokens, gate_up, down, expert_ids, gate_num):
    shards = lax.axis_size("dev")
    column_count = shards // EXPERTS
    tok_rows = tokens.shape[0]
    half_width = tokens.shape[1]
    depth, _, _, width = gate_up.shape
    flat_ids = expert_ids.reshape(-1)
    onehot = (flat_ids[:, None] == jnp.arange(EXPERTS, dtype=jnp.int32)[None, :]).astype(jnp.int32)
    earlier = jnp.cumsum(onehot, axis=0) - onehot
    slot_index = jnp.sum(earlier * onehot, axis=1)
    positions = (flat_ids * CAP + slot_index).reshape(tok_rows, TOP)
    numerators = gate_num.astype(jnp.float32)
    shares = numerators / jnp.sum(numerators, axis=1, keepdims=True)
    places = jnp.arange(EXPERTS * CAP, dtype=jnp.int32)
    matches = places[:, None, None] == positions[None, :, :]
    select = jnp.any(matches, axis=2).astype(jnp.bfloat16)
    combine = jnp.sum(jnp.where(matches, shares[None, :, :], 0.0), axis=2)

    outgoing = jnp.dot(select, tokens, preferred_element_type=jnp.float32).astype(jnp.bfloat16)
    copies = jnp.broadcast_to(
        outgoing.reshape(EXPERTS, 1, CAP, half_width), (EXPERTS, column_count, CAP, half_width)
    )
    received = lax.all_to_all(
        copies.reshape(shards, CAP, half_width), "dev", split_axis=0, concat_axis=0, tiled=True
    )
    total = shards * CAP
    chunks = chunk_count(width)
    by_target = jnp.transpose(gate_up, (2, 1, 0, 3))
    any_space = pl.BlockSpec(memory_space=pl.ANY)
    vmem_space = pl.BlockSpec(memory_space=pltpu.VMEM)
    flops = 2 * total * 3 * width * 2 * half_width
    keep, give = pl.pallas_call(
        functools.partial(expert_kernel, shards, chunks, EXPERTS * CAP),
        out_shape=[jax.ShapeDtypeStruct((total, half_width), jnp.float32)] * 2,
        in_specs=[any_space] * 3,
        out_specs=[vmem_space] * 2,
        scratch_shapes=[
            pltpu.VMEM((2, total, half_width), jnp.bfloat16),
            pltpu.VMEM((chunks, 2, shards * depth, width // chunks), jnp.bfloat16),
            pltpu.VMEM((2, width, half_width), jnp.bfloat16),
            pltpu.SemaphoreType.DMA((chunks,)),
            pltpu.SemaphoreType.DMA((chunks,)),
            pltpu.SemaphoreType.DMA((chunks,)),
            pltpu.SemaphoreType.DMA,
            pltpu.SemaphoreType.DMA,
            pltpu.SemaphoreType.DMA,
            pltpu.SemaphoreType.DMA((2,)),
        ],
        compiler_params=pltpu.CompilerParams(
            collective_id=0, has_side_effects=True, vmem_limit_bytes=67043328
        ),
        cost_estimate=pl.CostEstimate(
            flops=flops, bytes_accessed=2 * by_target.size * 2, transcendentals=total * width
        ),
    )(received.reshape(total, half_width), by_target, down)
    summed = keep + lax.ppermute(give, "grp", [(0, 1), (1, 0)])
    returned = lax.all_to_all(
        summed.astype(jnp.bfloat16).reshape(shards, CAP, half_width),
        "dev",
        split_axis=0,
        concat_axis=0,
        tiled=True,
    )
    expert_out = jnp.sum(
        returned.reshape(EXPERTS, column_count, CAP, half_width).astype(jnp.float32), axis=1
    ).reshape(EXPERTS * CAP, half_width)
    combined = jnp.dot(
        combine.T, expert_out, preferred_element_type=jnp.float32, precision=lax.Precision.HIGHEST
    )
    return combined.astype(jnp.bfloat16)


def solution(mesh):
    in_specs = (
        P("dev", "grp"),
        P("dev", None, None, "grp"),
        P("dev", "grp", None),
        P("dev", None),
        P("dev", None),
    )
    out_specs = P("dev", "grp")
    return jax.shard_map(local, mesh=mesh, in_specs=in_specs, out_specs=out_specs, check_vma=False)
```

time: 902 us -> 770 us (0.85)
  waiting for transfers between devices: 744 us -> 40.6 us
  Pallas kernels: 0 us -> 662 us
  matrix products: 47.7 us -> 3.07 us
  local copies, waits for them, and re-layouts: 70.8 us -> 30.9 us
  between operations: 13.5 us -> 0.09 us
    pallas_call x0 -> x1, Pallas kernels: none -> 662 us  [local(): pl.pallas_call(functools.partial(expert_kernel, shards, chunks, EXPERTS *...]
    all_to_all x3 -> x2, waiting for transfers between devices: 689 us -> 35.4 us  [the longest x1 31.5 us: local(): lax.all_to_all(summed.astype(jnp.bfloat16).reshape(shards, CAP, half_widt...]
    reduce_scatter x1 -> x0, waiting for transfers between devices: 54.7 us -> none  [local(): lax.psum_scatter(partial_value, 'grp', scatter_dimension=1, tiled=True)]
    dot_general x2 -> x0, matrix products: 45.6 us -> none  [the longest x1 26.1 us: project(): jnp.dot(row_block, received_block.reshape(received_block.shape[0], 2 * bl...]
    all_to_all x1 -> x0, local copies, waits for them, and re-layouts: 39.3 us -> none  [local(): lax.all_to_all(gate_up, 'dev', split_axis=2, concat_axis=0, tiled=True)]
    all_to_all x3 -> x2, starting transfers between devices: 19.9 us -> 27.4 us  [the longest x1 20.2 us: local(): lax.all_to_all(summed.astype(jnp.bfloat16).reshape(shards, CAP, half_widt...]
    unnamed x10 -> x8, local copies, waits for them, and re-layouts: 29.5 us -> 28.9 us
  transfers between devices with their start and end apart: 5 -> 3, of which waited for: 4 -> 3; matrix products, arithmetic and copies ran while one was open for 7% -> 4% of each run, Pallas kernels for 0% -> 0%
where the time goes in v1:
time: 770 us
  Pallas kernels  662 us (86%)
  waiting for transfers between devices  40.6 us (5%)
  local copies, waits for them, and re-layouts  30.9 us (4%)
  starting transfers between devices  27.5 us (4%)
    pallas_call x1, Pallas kernels, local(): pl.pallas_call(functools.partial(expert_kernel, shards, chunks, EXPERTS *...  662 us
    all_to_all x1, waiting for transfers between devices, local(): lax.all_to_all(summed.astype(jnp.bfloat16).reshape(shards, CAP, half_widt...  31.5 us
    unnamed x8, local copies, waits for them, and re-layouts  28.9 us
    all_to_all x1, starting transfers between devices, local(): lax.all_to_all(summed.astype(jnp.bfloat16).reshape(shards, CAP, half_widt...  20.2 us
  transfers between devices with their start and end apart: 3, of which 3 were waited for; matrix products, arithmetic and copies ran while one was open for 4% of the time, Pallas kernels for 0%

profile of v1, /device:TPU:8, one launch (start us, length us, event | category | flops | bytes accessed | tf_op | source)
XLA Modules:
  0.0 769.6 jit_solution(7630504543283846619)
XLA Ops:
  0.0 0.8 copy.21
  0.8 0.1 eq.43
  0.9 0.1 eq.39
  1.1 0.6 reduce-window.6
  1.7 0.2 slice_reduce_fusion
  1.9 0.1 fusion.2
  2.0 0.1 reduce_sum.39
  2.2 0.1 copy.23
  2.2 0.7 multiply_add_fusion
  2.9 0.0 copy-start
  2.9 0.6 copy-done
  3.5 1.3 convolution_convert_fusion
  4.8 1.3 broadcast_in_dim.26
  6.1 7.2 all-to-all-start
  13.4 27.6 %copy.26 = bf16[128,2,16,3584]{3,0,1,2:T(8,128)(2,1)} copy(bf16[128,2,16,3584]{3,2,1,0:T(8,128)(2,1)} %param.6) | data formatting | bytes 58720256 | tf_op args[1]
  40.9 4.0 all-to-all-done
  44.9 662.4 %shard_map.55 = (f32[640,1024]{1,0:T(8,128)}, f32[640,1024]{1,0:T(8,128)}) custom-call(bf16[640,1024]{1,0:T(8,128)(2,1)} %bitcast.4.routed_ref, bf16[16,2,128,3584]{3,2,1,0:T(8,128)(2,1)} %bitcast.23, bf16[1,3584,2048]{2,1,0:T(8,128)(2,1)} %down_ref.1), custom_call_target="tpu_custom_call" | custom-call | flops 28185722880 | bytes 58720256 | tf_op jit(solution)/shard_map/pallas_call | solution.py:194
  707.3 0.1 collective-permute-start
  707.4 5.1 collective-permute-done
  712.5 3.3 add_convert_fusion
  715.8 0.0 copy-start.2
  715.8 0.0 copy-start.1
  715.8 20.2 %all-to-all-start.1 = ((bf16[16,40,1024]{2,1,0:T(8,128)(2,1)}), bf16[16,40,1024]{2,1,0:T(8,128)(2,1)S(1)}, u32[]{:S(2)}, u32[]{:S(2)}) async-start(bf16[16,40,1024]{2,1,0:T(8,128)(2,1)} %bitcast.6), calls=%async_computation.1 | async-start | bytes 2621440 | tf_op jit(solution)/shard_map/all_to_all | solution.py:219
  736.0 0.0 copy-done.2
  736.0 0.0 copy-done.1
  736.0 31.5 %all-to-all-done.1 = bf16[16,40,1024]{2,1,0:T(8,128)(2,1)S(1)} async-done(((bf16[16,40,1024]{2,1,0:T(8,128)(2,1)}), bf16[16,40,1024]{2,1,0:T(8,128)(2,1)S(1)}, u32[]{:S(2)}, u32[]{:S(2)}) %all-to-all-start.1) | async-done | bytes 1310752 | tf_op jit(solution)/shard_map/all_to_all | solution.py:219
  767.5 0.3 convert_reduce_fusion
  767.8 1.8 convolution_convert_fusion.1
  (7 shorter events, 0.1 us)
Async XLA Ops:
  2.9 0.6 copy-start
  6.1 38.8 %all-to-all-start = ((bf16[16,40,1024]{2,1,0:T(8,128)(2,1)}), bf16[16,40,1024]{2,1,0:T(8,128)(2,1)}, u32[]{:S(2)}, u32[]{:S(2)}) async-start(bf16[16,40,1024]{2,1,0:T(8,128)(2,1)} %bitcast.3), calls=%async_computation | async-start | bytes 2621440 | tf_op jit(solution)/shard_map/all_to_all | solution.py:185
  707.3 5.2 collective-permute-start
  715.8 20.2 %copy-start.2 = (s32[128,2]{0,1:T(2,128)S(1)}, s32[128,2]{0,1:T(2,128)}, u32[]{:S(2)}) copy-start(s32[128,2]{0,1:T(2,128)} %param.9) | copy-start | bytes 3076
  715.8 20.2 %copy-start.1 = (s32[128,2]{0,1:T(2,128)S(1)}, s32[128,2]{0,1:T(2,128)}, u32[]{:S(2)}) copy-start(s32[128,2]{0,1:T(2,128)} %copy-done) | copy-start | bytes 3076
  715.8 51.8 %all-to-all-start.1 = ((bf16[16,40,1024]{2,1,0:T(8,128)(2,1)}), bf16[16,40,1024]{2,1,0:T(8,128)(2,1)S(1)}, u32[]{:S(2)}, u32[]{:S(2)}) async-start(bf16[16,40,1024]{2,1,0:T(8,128)(2,1)} %bitcast.6), calls=%async_computation.1 | async-start | bytes 2621440 | tf_op jit(solution)/shard_map/all_to_all | solution.py:219

commit v2 on v1

--- a/solution.py
+++ b/solution.py
@@ -70,9 +70,13 @@
     def place(owner):
         return pl.ds(pl.multiple_of(owner * depth, depth), depth)
 
+    def partner(step):
+        plane = lax.rem(me // 4 + step // 4, n // 4)
+        return plane * 4 + lax.rem(me // 2 + step // 2, 2) * 2 + lax.rem(me + step, 2)
+
     def send_chunk(chunk, carry):
         def send(step, inner):
-            target = lax.rem(me + step, n)
+            target = partner(step)
             pltpu.make_async_remote_copy(
                 src_ref=weights_ref.at[target, :, :, columns(chunk)],
                 dst_ref=landed.at[chunk, :, place(me), :],

time: 770 us -> 747 us (0.970)
  Pallas kernels: 662 us -> 645 us
    pallas_call x1, Pallas kernels: 662 us -> 645 us  [local(): pl.pallas_call(functools.partial(expert_kernel, shards, chunks, EXPERTS *...]
where the time goes in v2:
time: 747 us
  Pallas kernels  645 us (86%)
  waiting for transfers between devices  40.6 us (5%)
  local copies, waits for them, and re-layouts  30.9 us (4%)
  starting transfers between devices  21.7 us (3%)
    pallas_call x1, Pallas kernels, local(): pl.pallas_call(functools.partial(expert_kernel, shards, chunks, EXPERTS *...  645 us
    all_to_all x1, waiting for transfers between devices, local(): lax.all_to_all(summed.astype(jnp.bfloat16).reshape(shards, CAP, half_widt...  31.5 us
    unnamed x8, local copies, waits for them, and re-layouts  28.9 us
  transfers between devices with their start and end apart: 3, of which 3 were waited for; matrix products, arithmetic and copies ran while one was open for 4% of the time, Pallas kernels for 0%

profile of v2, /device:TPU:8, one launch (start us, length us, event | category | flops | bytes accessed | tf_op | source)
XLA Modules:
  0.0 746.5 jit_solution(4232755770211829748)
XLA Ops:
  0.0 0.8 copy.21
  0.8 0.1 eq.43
  0.9 0.1 eq.39
  1.1 0.6 reduce-window.6
  1.7 0.2 slice_reduce_fusion
  1.9 0.1 fusion.2
  2.0 0.1 reduce_sum.39
  2.2 0.1 copy.23
  2.2 0.7 multiply_add_fusion
  2.9 0.0 copy-start
  2.9 0.6 copy-done
  3.5 1.3 convolution_convert_fusion
  4.8 1.3 broadcast_in_dim.26
  6.1 7.2 all-to-all-start
  13.4 27.6 %copy.26 = bf16[128,2,16,3584]{3,0,1,2:T(8,128)(2,1)} copy(bf16[128,2,16,3584]{3,2,1,0:T(8,128)(2,1)} %param.6) | data formatting | bytes 58720256 | tf_op args[1]
  40.9 4.0 all-to-all-done
  44.9 645.1 %shard_map.55 = (f32[640,1024]{1,0:T(8,128)}, f32[640,1024]{1,0:T(8,128)}) custom-call(bf16[640,1024]{1,0:T(8,128)(2,1)} %bitcast.4.routed_ref, bf16[16,2,128,3584]{3,2,1,0:T(8,128)(2,1)} %bitcast.23, bf16[1,3584,2048]{2,1,0:T(8,128)(2,1)} %down_ref.1), custom_call_target="tpu_custom_call" | custom-call | flops 28185722880 | bytes 58720256 | tf_op jit(solution)/shard_map/pallas_call | solution.py:198
  690.0 0.1 collective-permute-start
  690.0 5.1 collective-permute-done
  695.1 3.3 add_convert_fusion
  698.4 0.0 copy-start.2
  698.4 0.0 copy-start.1
  698.4 14.4 %all-to-all-start.1 = ((bf16[16,40,1024]{2,1,0:T(8,128)(2,1)}), bf16[16,40,1024]{2,1,0:T(8,128)(2,1)S(1)}, u32[]{:S(2)}, u32[]{:S(2)}) async-start(bf16[16,40,1024]{2,1,0:T(8,128)(2,1)} %bitcast.6), calls=%async_computation.1 | async-start | bytes 2621440 | tf_op jit(solution)/shard_map/all_to_all | solution.py:223
  712.8 0.0 copy-done.2
  712.9 0.0 copy-done.1
  712.9 31.5 %all-to-all-done.1 = bf16[16,40,1024]{2,1,0:T(8,128)(2,1)S(1)} async-done(((bf16[16,40,1024]{2,1,0:T(8,128)(2,1)}), bf16[16,40,1024]{2,1,0:T(8,128)(2,1)S(1)}, u32[]{:S(2)}, u32[]{:S(2)}) %all-to-all-start.1) | async-done | bytes 1310752 | tf_op jit(solution)/shard_map/all_to_all | solution.py:223
  744.4 0.3 convert_reduce_fusion
  744.7 1.8 convolution_convert_fusion.1
  (7 shorter events, 0.1 us)
Async XLA Ops:
  2.9 0.6 copy-start
  6.1 38.8 %all-to-all-start = ((bf16[16,40,1024]{2,1,0:T(8,128)(2,1)}), bf16[16,40,1024]{2,1,0:T(8,128)(2,1)}, u32[]{:S(2)}, u32[]{:S(2)}) async-start(bf16[16,40,1024]{2,1,0:T(8,128)(2,1)} %bitcast.3), calls=%async_computation | async-start | bytes 2621440 | tf_op jit(solution)/shard_map/all_to_all | solution.py:189
  690.0 5.2 collective-permute-start
  698.4 14.4 %copy-start.2 = (s32[128,2]{0,1:T(2,128)S(1)}, s32[128,2]{0,1:T(2,128)}, u32[]{:S(2)}) copy-start(s32[128,2]{0,1:T(2,128)} %param.9) | copy-start | bytes 3076
  698.4 14.5 %copy-start.1 = (s32[128,2]{0,1:T(2,128)S(1)}, s32[128,2]{0,1:T(2,128)}, u32[]{:S(2)}) copy-start(s32[128,2]{0,1:T(2,128)} %copy-done) | copy-start | bytes 3076
  698.4 46.0 %all-to-all-start.1 = ((bf16[16,40,1024]{2,1,0:T(8,128)(2,1)}), bf16[16,40,1024]{2,1,0:T(8,128)(2,1)S(1)}, u32[]{:S(2)}, u32[]{:S(2)}) async-start(bf16[16,40,1024]{2,1,0:T(8,128)(2,1)} %bitcast.6), calls=%async_computation.1 | async-start | bytes 2621440 | tf_op jit(solution)/shard_map/all_to_all | solution.py:223
